TPU v7x, 256 devices: a 8x8x2 block of a 8x8x16 slice. The times are simulated.
256 devices in a mesh: groups: 2 (over z), attn: 16 (over y, core), expert: 8 (over x).
Axes of the slice: x: 8, y: 8, z: 2, core: 2. Of those that a mesh axis runs over, the one named last changes fastest.
The devices are a block of a 8x8x16 slice.
Arguments:
- tokens: bfloat16 [4096, 4096], P(('groups', 'attn'), 'expert'), parts along dimension 0, may hold values from -6 to 6
- expert_ids: int32 [4096, 8], P(('groups', 'attn')), parts along dimension 0, may hold values from 0 to 63, all different within a row; in each aligned block of 128 rows (0 to 127, 128 to 255, ...) at most 48 rows name the same one
- gate_weight: bfloat16 [4096, 8], P(('groups', 'attn')), parts along dimension 0, may hold values from 0.049804688 to 0.29882812
- w_gate: bfloat16 [64, 4096, 768], P('attn', 'expert'), may hold values from -0.09375 to 0.09375
- w_up: bfloat16 [64, 4096, 768], P('attn', 'expert'), may hold values from -0.09375 to 0.09375
- w_down: bfloat16 [64, 768, 4096], P('attn', None, 'expert'), may hold values from -0.21875 to 0.21875
- query: bfloat16 [512, 64, 128], P(('groups', 'attn', 'expert')), parts along dimension 0, may hold values from -100 to 100
- cache_k: bfloat16 [512, 768, 4, 128], P(('groups', 'attn', 'expert')), parts along dimension 0, may hold values from -6 to 6
- cache_v: bfloat16 [512, 768, 4, 128], P(('groups', 'attn', 'expert')), parts along dimension 0, may hold values from -6 to 6
- lengths: int32 [512], P(('groups', 'attn', 'expert')), parts along dimension 0, may hold values from 2 to 768, as said below
Outputs:
- moe_out: bfloat16 [4096, 4096], P(('groups', 'attn'), 'expert'), parts along dimension 0
- attn_out: bfloat16 [512, 8192], P(('groups', 'attn', 'expert')), parts along dimension 0
There are 2 independent parts, one for each index of `groups`. A program takes and returns all parts, laid end to end along the dimension named above; an argument that names none is the same for every part. Nothing has to cross between parts.
Inputs may be any that keep to these rules, and one draw needn't show every extreme that they name: `expert_ids`: each row names 8 different experts. In the rows of one index of attn (aligned blocks of 128 rows) no expert is named by more than 48 rows, and in some block some expert by exactly 48. `lengths`: some sequence has all 768 positions live.
All inputs are finite; a program needn't handle non-finite values.
Results may differ from a plain program's by a relative error of at most 0.025.
Values may be sent and summed in bfloat16 or wider, within the bound.
No kernel may reach another device: no remote copies, remote signals or barrier semaphores. Data moves between devices by JAX's collectives and lax.ppermute only.
A program may use at most 64 MiB of HBM per device.

v0:
```python
import jax
import jax.numpy as jnp
from jax import lax
from jax.sharding import PartitionSpec as P


def laid_out(tiles, dim):
    dims = list(tiles.shape[1:])
    dims[dim] *= tiles.shape[0]
    return jnp.moveaxis(tiles, 0, dim).reshape(dims)


def copy_for_each(shard, axis):
    count = lax.axis_size(axis)
    return lax.all_to_all(
        jnp.broadcast_to(shard[None], (count, *shard.shape)), axis, 0, 0, tiled=True
    )


def gather_directly(shard, axis, dim):
    return laid_out(copy_for_each(shard, axis), dim)


def member_table(expert_ids, experts):
    wanted = jnp.arange(experts, dtype=jnp.int32)
    return jnp.any(expert_ids[:, :, None] == wanted[None, None, :], axis=1).astype(jnp.int32)


def pad_rows(values):
    feat_width = values.shape[-1]
    flat_rows = values.reshape(-1, feat_width)
    return jnp.concatenate([flat_rows, jnp.zeros((1, feat_width), values.dtype)], axis=0)


def return_slots(results, starts_in, kept_in, slot_count):
    local_experts = results.shape[0]
    capacity = results.shape[1]
    slot_ids = jnp.arange(slot_count, dtype=jnp.int32)[None, None, :]
    column = jnp.arange(local_experts, dtype=jnp.int32)[None, :, None]
    row_index = column * capacity + starts_in[:, :, None] + slot_ids
    row_index = jnp.where(slot_ids < kept_in[:, :, None], row_index, local_experts * capacity)
    return pad_rows(results)[row_index]


def grouped_attention(query, cache_k, cache_v, lengths):
    seq_count, head_total, head_size = query.shape
    context = cache_k.shape[1]
    kv_count = cache_k.shape[2]
    grouped = query.reshape(seq_count, kv_count, head_total // kv_count, head_size)
    scores = jnp.einsum(
        "skgd,slkd->skgl", grouped, cache_k, preferred_element_type=jnp.float32
    ) * head_size ** (-0.5)
    live_mask = (
        lax.broadcasted_iota(jnp.int32, (seq_count, 1, 1, context), 3)
        < lengths[:, None, None, None]
    )
    masked = jnp.where(live_mask, scores, -jnp.inf)
    row_peak = jnp.max(masked, axis=3, keepdims=True)
    weighted = jnp.exp(masked - row_peak)
    denominator = jnp.sum(weighted, axis=3, keepdims=True)
    prob_bf = (weighted / denominator).astype(jnp.bfloat16)
    attended = jnp.einsum("skgl,slkd->skgd", prob_bf, cache_v, preferred_element_type=jnp.float32)
    return attended.reshape(seq_count, head_total * head_size).astype(jnp.bfloat16)


def body(tokens, expert_ids, gate_weight, w_gate, w_up, w_down, query, cache_k, cache_v, lengths):
    tok_rows, feat_width = tokens.shape
    top_count = expert_ids.shape[1]
    local_experts = w_gate.shape[0]
    ffn_width = w_gate.shape[2]
    attn_count = lax.axis_size("attn")
    experts = local_experts * attn_count
    capacity = tok_rows * top_count // local_experts
    slot_count = min(tok_rows, 3 * tok_rows * top_count // experts)
    member = member_table(expert_ids, experts)
    local_rank = jnp.cumsum(member, axis=0, dtype=jnp.int32) - member
    whole_ids = None
    whole_tokens, whole_ids, whole_gates = (
        gather_directly(tokens, "attn", 0),
        gather_directly(expert_ids, "attn", 0),
        gather_directly(gate_weight, "attn", 0),
    )
    all_rows = whole_tokens.shape[0]
    whole_member = member_table(whole_ids, experts)
    all_counts = jnp.sum(
        whole_member.reshape(attn_count, tok_rows, experts), axis=1, dtype=jnp.int32
    )
    src_offsets = jnp.cumsum(all_counts, axis=0, dtype=jnp.int32) - all_counts
    src_kept = jnp.clip(capacity - src_offsets, 0, all_counts)
    my_index = lax.axis_index("attn")
    offsets = lax.dynamic_index_in_dim(src_offsets, my_index, 0, keepdims=False)
    position = offsets[None, :] + local_rank
    starts_in = lax.dynamic_slice_in_dim(src_offsets, my_index * local_experts, local_experts, 1)
    kept_in = lax.dynamic_slice_in_dim(src_kept, my_index * local_experts, local_experts, 1)
    my_member = lax.dynamic_slice_in_dim(whole_member, my_index * local_experts, local_experts, 1)
    queue_place = jnp.cumsum(my_member, axis=0, dtype=jnp.int32) - my_member
    pack_target = jnp.where(
        (my_member > 0) & (queue_place < capacity),
        jnp.arange(local_experts, dtype=jnp.int32)[None, :] * capacity + queue_place,
        local_experts * capacity,
    )
    holders = jnp.broadcast_to(
        jnp.arange(all_rows, dtype=jnp.int32)[:, None], (all_rows, local_experts)
    )
    pack_index = (
        jnp.full((local_experts * capacity,), all_rows, jnp.int32)
        .at[pack_target.reshape(-1)]
        .set(holders.reshape(-1), mode="drop")
    )
    packed = pad_rows(whole_tokens)[pack_index].reshape(local_experts, capacity, feat_width)
    gate_part = jnp.einsum("jrd,jdf->jrf", packed, w_gate, preferred_element_type=jnp.float32)
    up_part = jnp.einsum("jrd,jdf->jrf", packed, w_up, preferred_element_type=jnp.float32)
    both_parts = jnp.concatenate([gate_part, up_part], axis=2)
    row_sums = lax.psum_scatter(
        both_parts.astype(jnp.bfloat16), "expert", scatter_dimension=1, tiled=True
    ).astype(jnp.float32)
    hidden_share = (jax.nn.silu(row_sums[:, :, :ffn_width]) * row_sums[:, :, ffn_width:]).astype(
        jnp.bfloat16
    )
    hidden = gather_directly(hidden_share, "expert", 1)
    results = jnp.einsum("jrf,jfd->jrd", hidden, w_down, preferred_element_type=jnp.float32).astype(
        jnp.bfloat16
    )
    back_rows = return_slots(results, starts_in, kept_in, slot_count)
    returned = lax.all_to_all(back_rows, "attn", split_axis=0, concat_axis=0, tiled=True)
    slot_of = jnp.take_along_axis(local_rank, expert_ids, axis=1)
    place_of = jnp.take_along_axis(position, expert_ids, axis=1)
    keep_mask = place_of < capacity
    picked = returned.reshape(experts * slot_count, feat_width)[expert_ids * slot_count + slot_of]
    factor = jnp.where(keep_mask, gate_weight.astype(jnp.float32), 0.0)
    moe_out = jnp.sum(factor[:, :, None] * picked.astype(jnp.float32), axis=1).astype(jnp.bfloat16)
    attn_out = grouped_attention(query, cache_k, cache_v, lengths)
    return (moe_out, attn_out)


def solution(mesh):
    return jax.shard_map(
        body,
        mesh=mesh,
        in_specs=(
            P(("groups", "attn"), "expert"),
            P(("groups", "attn"), None),
            P(("groups", "attn"), None),
            P("attn", "expert", None),
            P("attn", "expert", None),
            P("attn", None, "expert"),
            P(("groups", "attn", "expert"), None, None),
            P(("groups", "attn", "expert"), None, None, None),
            P(("groups", "attn", "expert"), None, None, None),
            P(("groups", "attn", "expert")),
        ),
        out_specs=(P(("groups", "attn"), "expert"), P(("groups", "attn", "expert"), None)),
        check_vma=False,
    )
```

profile of v0, /device:TPU:513, one launch (start us, length us, event | category | flops | bytes accessed | tf_op | source)
XLA Modules:
  0.0 318.8 jit_solution(7994495979518382753)
XLA Ops:
  7.2 0.8 broadcast_in_dim.36
  8.0 30.9 %all_to_all.20 = s32[16,128,8]{1,2,0:T(8,128)S(1)} all-to-all(s32[16,128,8]{1,2,0:T(8,128)S(1)} %broadcast_in_dim.36), channel_id=1, replica_groups=mesh['groups'=2,'attn'=16,'expert'=8] {'attn'}, dimensions={0} | all-to-all | bytes 131072 | tf_op jit(solution)/shard_map/all_to_all | solution.py:15
  38.9 2.5 broadcast_in_dim.39
  41.4 4.5 %all-to-all-start.1 = ((bf16[16,128,512]{2,1,0:T(8,128)(2,1)}), bf16[16,128,512]{2,1,0:T(8,128)(2,1)}, u32[]{:S(2)}, u32[]{:S(2)}) async-start(bf16[16,128,512]{2,1,0:T(8,128)(2,1)} %broadcast_in_dim.39), calls=%async_computation.1 | async-start | bytes 4194304 | tf_op jit(solution)/shard_map/all_to_all | solution.py:15
  45.9 0.1 reduce-scatter.2.cloned.1.call-start
  46.0 1.0 broadcast_in_dim.42
  47.0 1.8 reshape.197
  48.9 0.7 fusion.1
  49.6 0.9 convert_bitcast_fusion
  50.4 0.8 copy-done.3
  51.2 1.2 reduce-window.6
  52.4 0.2 slice_reduce_fusion
  52.6 0.2 reduce-window.9
  52.8 0.1 add_bitcast_fusion
  52.9 0.9 add_select_fusion
  53.8 1.3 copy.130
  55.2 2.0 reshape.148
  57.2 30.4 %scatter_custom_fusion = s32[1024]{0:T(1024)S(1)} fusion(s32[8192]{0:T(1024)S(1)} %bitcast.73, s32[8192]{0:T(1024)S(1)} %reshape.197, s32[]{:T(128)} %constant.35.clone.1), kind=kCustom, calls=%fused_computation.58 | custom fusion | bytes 4100 | tf_op jit(solution)/shard_map/scatter | solution.py:108
  87.6 7.5 %all-to-all-done.1 = bf16[16,128,512]{2,1,0:T(8,128)(2,1)} async-done(((bf16[16,128,512]{2,1,0:T(8,128)(2,1)}), bf16[16,128,512]{2,1,0:T(8,128)(2,1)}, u32[]{:S(2)}, u32[]{:S(2)}) %all-to-all-start.1) | async-done | bytes 2097184 | tf_op jit(solution)/shard_map/all_to_all | solution.py:15
  95.2 3.1 concatenate.10
  98.3 7.0 %gather_fusion = bf16[1024,512]{1,0:T(8,128)(2,1)} fusion(bf16[2049,512]{1,0:T(8,128)(2,1)} %concatenate.10, s32[1024]{0:T(1024)S(1)} %fusion.22), kind=kCustom, calls=%fused_computation.2 | custom fusion | bytes 2101248 | tf_op jit(solution)/shard_map/gather | solution.py:110
  105.3 2.4 convolution_convert_fusion
  107.7 0.1 copy-done.2
  107.8 1.0 convolution_convert_fusion.1
  108.8 1.9 pad_maximum_fusion
  110.7 0.1 reduce-scatter.2.cloned.1.call-update
  110.8 45.1 %reduce-scatter.2.cloned.1.call-done = bf16[4,32,1536]{2,1,0:T(8,128)(2,1)} async-done(((bf16[4,256,1536]{2,1,0:T(8,128)(2,1)}), bf16[4,32,1536]{2,1,0:T(8,128)(2,1)}) %reduce-scatter.2.cloned.1.call-update) | async-done | bytes 393232 | tf_op jit(solution)/shard_map/reduce_scatter | solution.py:114
  155.9 1.1 convert_element_type.45
  157.0 0.1 fusion.18
  157.1 1.3 broadcast_in_dim.48
  158.4 5.5 %all-to-all-start.2 = ((bf16[8,4,32,768]{3,2,1,0:T(8,128)(2,1)}), bf16[8,4,32,768]{3,2,1,0:T(8,128)(2,1)}, u32[]{:S(2)}, u32[]{:S(2)}) async-start(bf16[8,4,32,768]{3,2,1,0:T(8,128)(2,1)} %broadcast_in_dim.48), calls=%async_computation.3 | async-start | bytes 3145728 | tf_op jit(solution)/shard_map/all_to_all | solution.py:15
  164.0 1.9 copy.138
  165.9 2.2 reduce_sum.27
  168.1 0.1 copy.124
  168.2 0.1 dynamic-slice_minimum_fusion
  168.3 0.1 compare_select_fusion.1
  168.4 0.1 reshape.179
  168.5 33.4 %all-to-all-done.2 = bf16[8,4,32,768]{3,2,1,0:T(8,128)(2,1)} async-done(((bf16[8,4,32,768]{3,2,1,0:T(8,128)(2,1)}), bf16[8,4,32,768]{3,2,1,0:T(8,128)(2,1)}, u32[]{:S(2)}, u32[]{:S(2)}) %all-to-all-start.2) | async-done | bytes 1572896 | tf_op jit(solution)/shard_map/all_to_all | solution.py:15
  201.9 1.7 copy.131
  203.6 0.7 copy-done.8
  204.3 1.0 convolution_convert_fusion.2
  205.2 1.1 concatenate.12
  206.3 14.7 %gather_fusion.1 = bf16[3072,512]{1,0:T(8,128)(2,1)} fusion(bf16[1025,512]{1,0:T(8,128)(2,1)} %concatenate.12, s32[3072]{0:T(1024)S(1)} %broadcast_clamp_fusion), kind=kCustom, calls=%fused_computation.3 | custom fusion | bytes 6303744 | tf_op jit(solution)/shard_map/gather | solution.py:42
  221.0 9.9 %all-to-all-start.3 = ((bf16[16,4,48,512]{3,2,1,0:T(8,128)(2,1)}), bf16[16,4,48,512]{3,2,1,0:T(8,128)(2,1)}, u32[]{:S(2)}, u32[]{:S(2)}) async-start(bf16[16,4,48,512]{3,2,1,0:T(8,128)(2,1)} %bitcast.65), calls=%async_computation.4 | async-start | bytes 6291456 | tf_op jit(solution)/shard_map/all_to_all | solution.py:125
  230.9 0.1 copy.126
  231.1 0.1 copy.127
  231.2 0.1 reshape.217
  231.3 0.8 reduce_window_sum.38
  232.1 0.1 iota_compare_fusion.3
  232.1 1.9 fusion.12
  234.1 0.8 fusion.27
  234.9 2.5 fusion.15
  237.4 1.4 copy.157
  238.8 0.9 broadcast_add_fusion
  239.6 7.1 %gather_fusion.3 = s32[1024]{0:T(1024)S(1)} fusion(s32[128,64]{1,0:T(8,128)S(1)} %get-tuple-element.3, s32[1024]{0:T(1024)S(1)} %reshape.217), kind=kCustom, calls=%fused_computation.clone | custom fusion | bytes 16384 | tf_op jit(solution)/shard_map/jit(take_along_axis)/gather | solution.py:127
  246.7 7.1 %gather_fusion.4 = s32[1024]{0:T(1024)S(1)} fusion(s32[128,64]{1,0:T(8,128)S(1)} %get-tuple-element.4, s32[1024]{0:T(1024)S(1)} %reshape.217), kind=kCustom, calls=%fused_computation.1.clone | custom fusion | bytes 16384 | tf_op jit(solution)/shard_map/jit(take_along_axis)/gather | solution.py:126
  253.8 0.1 reshape.225
  254.0 0.1 copy.135
  254.1 0.1 reshape.187
  254.2 0.1 reshape.220
  254.3 0.1 copy.129
  254.5 47.5 %all-to-all-done.3 = bf16[16,4,48,512]{3,2,1,0:T(8,128)(2,1)} async-done(((bf16[16,4,48,512]{3,2,1,0:T(8,128)(2,1)}), bf16[16,4,48,512]{3,2,1,0:T(8,128)(2,1)}, u32[]{:S(2)}, u32[]{:S(2)}) %all-to-all-start.3) | async-done | bytes 3145760 | tf_op jit(solution)/shard_map/all_to_all | solution.py:125
  301.9 7.4 %gather_fusion.2 = bf16[1024,512]{1,0:T(8,128)(2,1)} fusion(bf16[3072,512]{1,0:T(8,128)(2,1)} %bitcast.12, s32[1024]{0:T(1024)S(1)} %broadcast_clamp_fusion.1), kind=kCustom, calls=%fused_computation.4 | custom fusion | bytes 2101248 | tf_op jit(solution)/shard_map/gather | solution.py:129
  309.3 2.6 fusion.2
  (32 shorter events, 0.3 us)
Async XLA Ops:
  7.2 98.1 %copy-start = (bf16[4,512,768]{2,1,0:T(8,128)(2,1)S(1)}, bf16[4,512,768]{2,1,0:T(8,128)(2,1)}, u32[]{:S(2)}) copy-start(bf16[4,512,768]{2,1,0:T(8,128)(2,1)} %param.16) | copy-start | bytes 9437188
  41.4 53.8 %all-to-all-start.1 = ((bf16[16,128,512]{2,1,0:T(8,128)(2,1)}), bf16[16,128,512]{2,1,0:T(8,128)(2,1)}, u32[]{:S(2)}, u32[]{:S(2)}) async-start(bf16[16,128,512]{2,1,0:T(8,128)(2,1)} %broadcast_in_dim.39), calls=%async_computation.1 | async-start | bytes 4194304 | tf_op jit(solution)/shard_map/all_to_all | solution.py:15
  45.9 110.0 %reduce-scatter.2.cloned.1.call-start = ((), (), s32[]{:S(2)}) async-start(), calls=%async_computation.5 | async-start | bytes 3538944 | tf_op jit(solution)/shard_map/reduce_scatter | solution.py:114
  50.4 0.8 copy-start.3
  105.3 2.4 copy-start.1
  105.3 2.5 copy-start.2
  158.4 43.5 %all-to-all-start.2 = ((bf16[8,4,32,768]{3,2,1,0:T(8,128)(2,1)}), bf16[8,4,32,768]{3,2,1,0:T(8,128)(2,1)}, u32[]{:S(2)}, u32[]{:S(2)}) async-start(bf16[8,4,32,768]{3,2,1,0:T(8,128)(2,1)} %broadcast_in_dim.48), calls=%async_computation.3 | async-start | bytes 3145728 | tf_op jit(solution)/shard_map/all_to_all | solution.py:15
  201.9 2.4 copy-start.8
  221.0 9.9 %copy-start.5 = (s32[128,8]{0,1:T(8,128)S(1)}, s32[128,8]{0,1:T(8,128)}, u32[]{:S(2)}) copy-start(s32[128,8]{0,1:T(8,128)} %param.13) | copy-start | bytes 12292
  221.0 11.1 %copy-start.7 = (s32[2]{0:T(128)S(1)}, s32[2]{0:T(128)}, u32[]{:S(2)}) copy-start(s32[2]{0:T(128)} %param.21) | copy-start | bytes 28
  221.0 80.9 %all-to-all-start.3 = ((bf16[16,4,48,512]{3,2,1,0:T(8,128)(2,1)}), bf16[16,4,48,512]{3,2,1,0:T(8,128)(2,1)}, u32[]{:S(2)}, u32[]{:S(2)}) async-start(bf16[16,4,48,512]{3,2,1,0:T(8,128)(2,1)} %bitcast.65), calls=%async_computation.4 | async-start | bytes 6291456 | tf_op jit(solution)/shard_map/all_to_all | solution.py:125
  231.0 1.1 copy-start.4
  246.7 7.6 %copy-start.6 = (bf16[128,8]{0,1:T(8,128)(2,1)S(1)}, bf16[128,8]{0,1:T(8,128)(2,1)}, u32[]{:S(2)}) copy-start(bf16[128,8]{0,1:T(8,128)(2,1)} %param.14) | copy-start | bytes 6148
Sparse Core Ops, SparseCore 0:
  110.9 44.9 reduce-scatter.1
where the time goes:
time: 320 us; the launch traced here: 319 us
  waiting for transfers between devices  134 us (42%)
  local copies, waits for them, and re-layouts  96.5 us (30%)
  blocking collectives  30.9 us (10%)
  starting transfers between devices  20 us (6%)
  other arithmetic  14.7 us (5%)
  between operations  14.3 us (4%)
  matrix products  8.71 us (3%)
    all_to_all x1, waiting for transfers between devices, body(): lax.all_to_all(back_rows, 'attn', split_axis=0, concat_axis=0, tiled=True)  47.5 us
    reduce_scatter x1, waiting for transfers between devices, body(): lax.psum_scatter(both_parts.astype(jnp.bfloat16), 'expert', scatter_dimen...  45.1 us
    all_to_all x2, waiting for transfers between devices, copy_for_each(): lax.all_to_all(jnp.broadcast_to(shard[None], (count, *shard.shape)), axis...  40.9 us
    all_to_all x1, blocking collectives, copy_for_each(): lax.all_to_all(jnp.broadcast_to(shard[None], (count, *shard.shape)), axis...  30.9 us
    scatter x1, local copies, waits for them, and re-layouts, body(): pack_index = jnp.full((local_experts * capacity,), all_rows, jnp.int32).a...  30.4 us
    gather x1, local copies, waits for them, and re-layouts, return_slots(): return pad_rows(results)[row_index]  14.7 us
    all_to_all x2, starting transfers between devices, copy_for_each(): lax.all_to_all(jnp.broadcast_to(shard[None], (count, *shard.shape)), axis...  10.1 us
    all_to_all x1, starting transfers between devices, body(): lax.all_to_all(back_rows, 'attn', split_axis=0, concat_axis=0, tiled=True)  9.88 us
  transfers between devices with their start and end apart: 4, of which 4 were waited for; matrix products, arithmetic and copies ran while one was open for 22% of the time, Pallas kernels for 0%

commit v1 on v0

--- a/solution.py
+++ b/solution.py
@@ -2,6 +2,17 @@
 import jax.numpy as jnp
 from jax import lax
 from jax.sharding import PartitionSpec as P
+
+
+def cut_along(x, dim, size):
+    before, after = (x.shape[:dim], x.shape[dim + 1 :])
+    return jnp.moveaxis(x.reshape(*before, size, -1, *after), dim, 0)
+
+
+def joined_along(blocks, dim):
+    shape = list(blocks.shape[1:])
+    shape[dim] *= blocks.shape[0]
+    return jnp.moveaxis(blocks, 0, dim).reshape(shape)
 
 
 def laid_out(tiles, dim):
@@ -122,7 +133,14 @@
         jnp.bfloat16
     )
     back_rows = return_slots(results, starts_in, kept_in, slot_count)
-    returned = lax.all_to_all(back_rows, "attn", split_axis=0, concat_axis=0, tiled=True)
+    size, place = (lax.axis_size("attn"), lax.axis_index("attn"))
+    blocks = cut_along(back_rows, 0, size)
+    gathered = [blocks[place]]
+    for step in range(1, size):
+        sent = blocks[place ^ step]
+        gathered.append(lax.ppermute(sent, "attn", [(i, i ^ step) for i in range(size)]))
+    blocks = jnp.stack(gathered)[place ^ jnp.arange(size)]
+    returned = joined_along(blocks, 0)
     slot_of = jnp.take_along_axis(local_rank, expert_ids, axis=1)
     place_of = jnp.take_along_axis(position, expert_ids, axis=1)
     keep_mask = place_of < capacity

time: 320 us -> 359 us (1.12)
  starting transfers between devices: 20 us -> 54.6 us
  local copies, waits for them, and re-layouts: 96.5 us -> 118 us
  waiting for transfers between devices: 134 us -> 117 us
    ppermute x0 -> x15, waiting for transfers between devices: none -> 55.2 us  [body(): lax.ppermute(sent, 'attn', [(i, i ^ step) for i in range(size)])]
    all_to_all x1 -> x0, waiting for transfers between devices: 47.5 us -> none  [body(): lax.all_to_all(back_rows, 'attn', split_axis=0, concat_axis=0, tiled=True)]
    ppermute x0 -> x15, starting transfers between devices: none -> 44.7 us  [body(): lax.ppermute(sent, 'attn', [(i, i ^ step) for i in range(size)])]
    all_to_all x2, waiting for transfers between devices: 40.9 us -> 18.5 us  [copy_for_each(): lax.all_to_all(jnp.broadcast_to(shard[None], (count, *shard.shape)), axis...]
    unnamed x22 -> x41, local copies, waits for them, and re-layouts: 5.01 us -> 17.8 us
    all_to_all x1 -> x0, starting transfers between devices: 9.88 us -> none  [body(): lax.all_to_all(back_rows, 'attn', split_axis=0, concat_axis=0, tiled=True)]
    gather x0 -> x1, local copies, waits for them, and re-layouts: none -> 4.3 us  [body(): blocks = jnp.stack(gathered)[place ^ jnp.arange(size)]]
  transfers between devices with their start and end apart: 4 -> 18, of which waited for: 4 -> 12; matrix products, arithmetic and copies ran while one was open for 22% -> 22% of each run, Pallas kernels for 0% -> 0%
where the time goes in v1:
time: 359 us; the launch traced here: 358 us
  local copies, waits for them, and re-layouts  118 us (33%)
  waiting for transfers between devices  117 us (33%)
  starting transfers between devices  54.6 us (15%)
  blocking collectives  30.9 us (9%)
  between operations  14.4 us (4%)
  other arithmetic  14.1 us (4%)
  matrix products  8.71 us (2%)
    ppermute x15, waiting for transfers between devices, body(): lax.ppermute(sent, 'attn', [(i, i ^ step) for i in range(size)])  55.2 us
    ppermute x15, starting transfers between devices, body(): lax.ppermute(sent, 'attn', [(i, i ^ step) for i in range(size)])  44.7 us
    reduce_scatter x1, waiting for transfers between devices, body(): lax.psum_scatter(both_parts.astype(jnp.bfloat16), 'expert', scatter_dimen...  43.4 us
    all_to_all x1, blocking collectives, copy_for_each(): lax.all_to_all(jnp.broadcast_to(shard[None], (count, *shard.shape)), axis...  30.9 us
    scatter x1, local copies, waits for them, and re-layouts, body(): pack_index = jnp.full((local_experts * capacity,), all_rows, jnp.int32).a...  30.4 us
    all_to_all x2, waiting for transfers between devices, copy_for_each(): lax.all_to_all(jnp.broadcast_to(shard[None], (count, *shard.shape)), axis...  18.5 us
    unnamed x41, local copies, waits for them, and re-layouts  17.8 us
    gather x1, local copies, waits for them, and re-layouts, return_slots(): return pad_rows(results)[row_index]  14.7 us
  transfers between devices with their start and end apart: 18, of which 12 were waited for; matrix products, arithmetic and copies ran while one was open for 22% of the time, Pallas kernels for 0%

profile of v1, /device:TPU:513, one launch (start us, length us, event | category | flops | bytes accessed | tf_op | source)
XLA Modules:
  0.0 357.7 jit_solution(14303782796586033204)
XLA Ops:
  7.2 0.8 broadcast_in_dim.36
  8.0 30.9 %all_to_all.15 = s32[16,128,8]{1,2,0:T(8,128)S(1)} all-to-all(s32[16,128,8]{1,2,0:T(8,128)S(1)} %broadcast_in_dim.36), channel_id=1, replica_groups=mesh['groups'=2,'attn'=16,'expert'=8] {'attn'}, dimensions={0} | all-to-all | bytes 131072 | tf_op jit(solution)/shard_map/all_to_all | solution.py:26
  38.9 2.5 broadcast_in_dim.39
  41.4 4.5 %all-to-all-start.1 = ((bf16[16,128,512]{2,1,0:T(8,128)(2,1)}), bf16[16,128,512]{2,1,0:T(8,128)(2,1)}, u32[]{:S(2)}, u32[]{:S(2)}) async-start(bf16[16,128,512]{2,1,0:T(8,128)(2,1)} %broadcast_in_dim.39), calls=%async_computation.1 | async-start | bytes 4194304 | tf_op jit(solution)/shard_map/all_to_all | solution.py:26
  46.0 1.0 broadcast_in_dim.42
  47.0 1.8 reshape.251
  49.6 0.9 convert_bitcast_fusion
  50.4 0.8 copy-done.3
  51.2 1.2 reduce-window.6
  52.9 0.9 add_select_fusion
  53.8 1.3 copy.130
  55.2 2.0 reshape.193
  57.2 30.4 %scatter_custom_fusion = s32[1024]{0:T(1024)S(1)} fusion(s32[8192]{0:T(1024)S(1)} %bitcast.109, s32[8192]{0:T(1024)S(1)} %reshape.251, s32[]{:T(128)} %constant.49.clone.1), kind=kCustom, calls=%fused_computation.93 | custom fusion | bytes 4100 | tf_op jit(solution)/shard_map/scatter | solution.py:119
  87.6 7.5 %all-to-all-done.1 = bf16[16,128,512]{2,1,0:T(8,128)(2,1)} async-done(((bf16[16,128,512]{2,1,0:T(8,128)(2,1)}), bf16[16,128,512]{2,1,0:T(8,128)(2,1)}, u32[]{:S(2)}, u32[]{:S(2)}) %all-to-all-start.1) | async-done | bytes 2097184 | tf_op jit(solution)/shard_map/all_to_all | solution.py:26
  95.2 3.1 concatenate.10
  98.3 7.0 %gather_fusion = bf16[1024,512]{1,0:T(8,128)(2,1)} fusion(bf16[2049,512]{1,0:T(8,128)(2,1)} %concatenate.10, s32[1024]{0:T(1024)S(1)} %fusion.22), kind=kCustom, calls=%fused_computation.2 | custom fusion | bytes 2101248 | tf_op jit(solution)/shard_map/gather | solution.py:121
  105.3 2.4 convolution_convert_fusion
  107.8 1.0 convolution_convert_fusion.1
  108.8 1.9 pad_maximum_fusion
  111.6 0.8 reduce_window_sum.38
  112.4 43.4 %reduce-scatter.2.cloned.1.call-done = bf16[4,32,1536]{2,1,0:T(8,128)(2,1)} async-done(((bf16[4,256,1536]{2,1,0:T(8,128)(2,1)}), bf16[4,32,1536]{2,1,0:T(8,128)(2,1)}) %reduce-scatter.2.cloned.1.call-update) | async-done | bytes 393232 | tf_op jit(solution)/shard_map/reduce_scatter | solution.py:125
  155.8 1.1 convert_element_type.45
  157.0 1.3 broadcast_in_dim.44
  158.3 5.3 %all-to-all-start.2 = ((bf16[8,4,32,768]{3,2,1,0:T(8,128)(2,1)}), bf16[8,4,32,768]{3,2,1,0:T(8,128)(2,1)}, u32[]{:S(2)}, u32[]{:S(2)}) async-start(bf16[8,4,32,768]{3,2,1,0:T(8,128)(2,1)} %broadcast_in_dim.44), calls=%async_computation.3 | async-start | bytes 3145728 | tf_op jit(solution)/shard_map/all_to_all | solution.py:26
  164.0 1.9 fusion.12
  166.2 2.5 fusion.15
  168.6 1.4 copy.157
  170.0 1.9 copy.138
  171.9 2.2 reduce_sum.27
  174.5 0.9 broadcast_add_fusion
  175.4 7.1 %gather_fusion.5 = s32[1024]{0:T(1024)S(1)} fusion(s32[128,64]{1,0:T(8,128)S(1)} %get-tuple-element.4, s32[1024]{0:T(1024)S(1)} %reshape.272), kind=kCustom, calls=%fused_computation.1.clone | custom fusion | bytes 16384 | tf_op jit(solution)/shard_map/jit(take_along_axis)/gather | solution.py:144
  182.9 7.1 %gather_fusion.4 = s32[1024]{0:T(1024)S(1)} fusion(s32[128,64]{1,0:T(8,128)S(1)} %get-tuple-element.3, s32[1024]{0:T(1024)S(1)} %reshape.272), kind=kCustom, calls=%fused_computation.clone | custom fusion | bytes 16384 | tf_op jit(solution)/shard_map/jit(take_along_axis)/gather | solution.py:145
  190.1 10.9 %all-to-all-done.2 = bf16[8,4,32,768]{3,2,1,0:T(8,128)(2,1)} async-done(((bf16[8,4,32,768]{3,2,1,0:T(8,128)(2,1)}), bf16[8,4,32,768]{3,2,1,0:T(8,128)(2,1)}, u32[]{:S(2)}, u32[]{:S(2)}) %all-to-all-start.2) | async-done | bytes 1572896 | tf_op jit(solution)/shard_map/all_to_all | solution.py:26
  201.0 1.7 copy.131
  203.4 1.0 convolution_convert_fusion.2
  204.4 1.1 concatenate.12
  205.4 14.7 %gather_fusion.1 = bf16[3072,512]{1,0:T(8,128)(2,1)} fusion(bf16[1025,512]{1,0:T(8,128)(2,1)} %concatenate.12, s32[3072]{0:T(1024)S(1)} %broadcast_clamp_fusion), kind=kCustom, calls=%fused_computation.3 | custom fusion | bytes 6303744 | tf_op jit(solution)/shard_map/gather | solution.py:53
  220.1 3.5 constant_dynamic-slice_fusion
  223.6 3.8 %collective-permute-start = (bf16[1,4,48,512]{3,2,1,0:T(8,128)(2,1)}, bf16[1,4,48,512]{3,2,1,0:T(8,128)(2,1)}, u32[]{:S(2)}, u32[]{:S(2)}) collective-permute-start(bf16[1,4,48,512]{3,2,1,0:T(8,128)(2,1)} %get-tuple-element.19), channel_id=1, source_target_pairs={{0,8},{8,0},{16,24},{24,16},{32,40},{40,32},{48,56},{56,48},{64,72... | collective-permute-start | bytes 589832 | tf_op jit(solution)/shard_map/ppermute | solution.py:141
  227.5 1.5 collective-permute-start.1
  229.3 2.3 collective-permute-start.3
  232.1 1.6 bitcast_dynamic-update-slice_fusion.15
  233.7 3.5 collective-permute-start.5
  237.2 1.6 bitcast_dynamic-update-slice_fusion.14
  238.8 3.3 collective-permute-done.1
  242.1 2.5 collective-permute-start.6
  245.3 1.2 collective-permute-done.2
  246.5 4.0 %collective-permute-start.7 = (bf16[1,4,48,512]{3,2,1,0:T(8,128)(2,1)}, bf16[1,4,48,512]{3,2,1,0:T(8,128)(2,1)S(1)}, u32[]{:S(2)}, u32[]{:S(2)}) collective-permute-start(bf16[1,4,48,512]{3,2,1,0:T(8,128)(2,1)} %get-tuple-element.12), channel_id=1, source_target_pairs={{0,64},{8,72},{16,80},{24,88},{32,96},{40,104},{48,112},{56,120},{... | collective-permute-start | bytes 589832 | tf_op jit(solution)/shard_map/ppermute | solution.py:141
  251.2 1.8 collective-permute-start.8
  253.6 16.6 %collective-permute-done.4 = bf16[1,4,48,512]{3,2,1,0:T(8,128)(2,1)S(1)} collective-permute-done((bf16[1,4,48,512]{3,2,1,0:T(8,128)(2,1)}, bf16[1,4,48,512]{3,2,1,0:T(8,128)(2,1)S(1)}, u32[]{:S(2)}, u32[]{:S(2)}) %collective-permute-start.4) | collective-permute-done | bytes 196640 | tf_op jit(solution)/shard_map/ppermute | solution.py:141
  270.9 18.3 %collective-permute-start.10 = (bf16[1,4,48,512]{3,2,1,0:T(8,128)(2,1)}, bf16[1,4,48,512]{3,2,1,0:T(8,128)(2,1)S(1)}, u32[]{:S(2)}, u32[]{:S(2)}) collective-permute-start(bf16[1,4,48,512]{3,2,1,0:T(8,128)(2,1)} %get-tuple-element.9), channel_id=1, source_target_pairs={{0,88},{8,80},{16,72},{24,64},{32,120},{40,112},{48,104},{56,96},{... | collective-permute-start | bytes 589832 | tf_op jit(solution)/shard_map/ppermute | solution.py:141
  289.8 1.4 collective-permute-start.11
  291.9 1.2 collective-permute-start.12
  295.5 3.2 collective-permute-start.14
  299.4 17.5 %collective-permute-done.10 = bf16[1,4,48,512]{3,2,1,0:T(8,128)(2,1)S(1)} collective-permute-done((bf16[1,4,48,512]{3,2,1,0:T(8,128)(2,1)}, bf16[1,4,48,512]{3,2,1,0:T(8,128)(2,1)S(1)}, u32[]{:S(2)}, u32[]{:S(2)}) %collective-permute-start.10) | collective-permute-done | bytes 196640 | tf_op jit(solution)/shard_map/ppermute | solution.py:141
  317.6 3.5 collective-permute-done.11
  321.8 3.4 collective-permute-done.12
  325.9 6.4 %collective-permute-done.13 = bf16[1,4,48,512]{3,2,1,0:T(8,128)(2,1)S(1)} collective-permute-done((bf16[1,4,48,512]{3,2,1,0:T(8,128)(2,1)S(1)}, bf16[1,4,48,512]{3,2,1,0:T(8,128)(2,1)S(1)}, u32[]{:S(2)}, u32[]{:S(2)}) %collective-permute-start.13) | collective-permute-done | bytes 196640 | tf_op jit(solution)/shard_map/ppermute | solution.py:141
  332.3 0.7 bitcast_dynamic-update-slice_fusion.1
  333.1 2.8 collective-permute-done.14
  335.9 0.7 bitcast_dynamic-update-slice_fusion
  336.6 4.3 %gather_fusion.2 = bf16[16,4,48,512]{3,2,1,0:T(8,128)(2,1)} fusion(bf16[16,4,48,512]{3,2,1,0:T(8,128)(2,1)} %bitcast.28, s32[1024]{0:T(1024)S(1)} %pad_clamp_fusion), kind=kCustom, calls=%fused_computation.4 | custom fusion | bytes 6291520 | tf_op jit(solution)/shard_map/gather | solution.py:142
  340.9 7.4 %gather_fusion.3 = bf16[1024,512]{1,0:T(8,128)(2,1)} fusion(bf16[3072,512]{1,0:T(8,128)(2,1)} %bitcast.97, s32[1024]{0:T(1024)S(1)} %broadcast_clamp_fusion.1), kind=kCustom, calls=%fused_computation.5 | custom fusion | bytes 2101248 | tf_op jit(solution)/shard_map/gather | solution.py:147
  348.3 2.6 fusion.2
  (84 shorter events, 14.7 us)
Async XLA Ops:
  7.2 98.1 %copy-start = (bf16[4,512,768]{2,1,0:T(8,128)(2,1)S(1)}, bf16[4,512,768]{2,1,0:T(8,128)(2,1)}, u32[]{:S(2)}) copy-start(bf16[4,512,768]{2,1,0:T(8,128)(2,1)} %param.16) | copy-start | bytes 9437188
  41.4 53.8 %all-to-all-start.1 = ((bf16[16,128,512]{2,1,0:T(8,128)(2,1)}), bf16[16,128,512]{2,1,0:T(8,128)(2,1)}, u32[]{:S(2)}, u32[]{:S(2)}) async-start(bf16[16,128,512]{2,1,0:T(8,128)(2,1)} %broadcast_in_dim.39), calls=%async_computation.1 | async-start | bytes 4194304 | tf_op jit(solution)/shard_map/all_to_all | solution.py:26
  45.9 109.9 %reduce-scatter.2.cloned.1.call-start = ((), (), s32[]{:S(2)}) async-start(), calls=%async_computation.4 | async-start | bytes 3538944 | tf_op jit(solution)/shard_map/reduce_scatter | solution.py:125
  50.4 0.8 copy-start.3
  105.3 2.4 copy-start.1
  105.3 2.5 copy-start.2
  110.7 0.7 copy-start.7
  111.6 46.7 %copy-start.6 = (pred[128,64]{1,0:T(8,128)(4,1)}, pred[128,64]{1,0:T(8,128)(4,1)S(1)}, u32[]{:S(2)}) copy-start(pred[128,64]{1,0:T(8,128)(4,1)S(1)} %copy.126) | copy-start | bytes 24580
  156.9 7.0 %copy-start.9 = (s32[2]{0:T(128)S(1)}, s32[2]{0:T(128)}, u32[]{:S(2)}) copy-start(s32[2]{0:T(128)} %param.21) | copy-start | bytes 28
  158.3 42.7 %all-to-all-start.2 = ((bf16[8,4,32,768]{3,2,1,0:T(8,128)(2,1)}), bf16[8,4,32,768]{3,2,1,0:T(8,128)(2,1)}, u32[]{:S(2)}, u32[]{:S(2)}) async-start(bf16[8,4,32,768]{3,2,1,0:T(8,128)(2,1)} %broadcast_in_dim.44), calls=%async_computation.3 | async-start | bytes 3145728 | tf_op jit(solution)/shard_map/all_to_all | solution.py:26
  182.8 7.2 %copy-start.8 = (bf16[128,8]{0,1:T(8,128)(2,1)S(1)}, bf16[128,8]{0,1:T(8,128)(2,1)}, u32[]{:S(2)}) copy-start(bf16[128,8]{0,1:T(8,128)(2,1)} %param.14) | copy-start | bytes 6148
  201.0 2.4 copy-start.10
  223.6 10.1 %collective-permute-start = (bf16[1,4,48,512]{3,2,1,0:T(8,128)(2,1)}, bf16[1,4,48,512]{3,2,1,0:T(8,128)(2,1)}, u32[]{:S(2)}, u32[]{:S(2)}) collective-permute-start(bf16[1,4,48,512]{3,2,1,0:T(8,128)(2,1)} %get-tuple-element.19), channel_id=1, source_target_pairs={{0,8},{8,0},{16,24},{24,16},{32,40},{40,32},{48,56},{56,48},{64,72... | collective-permute-start | bytes 589832 | tf_op jit(solution)/shard_map/ppermute | solution.py:141
  227.4 64.4 %copy-start.5 = (bf16[1,4,48,512]{3,2,1,0:T(8,128)(2,1)S(1)}, bf16[1,4,48,512]{3,2,1,0:T(8,128)(2,1)}, u32[]{:S(2)}) copy-start(bf16[1,4,48,512]{3,2,1,0:T(8,128)(2,1)} %get-tuple-element.7) | copy-start | bytes 589828
  227.5 66.3 %copy-start.4 = (bf16[1,4,48,512]{3,2,1,0:T(8,128)(2,1)S(1)}, bf16[1,4,48,512]{3,2,1,0:T(8,128)(2,1)}, u32[]{:S(2)}) copy-start(bf16[1,4,48,512]{3,2,1,0:T(8,128)(2,1)} %get-tuple-element.6) | copy-start | bytes 589828
  227.5 14.6 %collective-permute-start.1 = (bf16[1,4,48,512]{3,2,1,0:T(8,128)(2,1)}, bf16[1,4,48,512]{3,2,1,0:T(8,128)(2,1)S(1)}, u32[]{:S(2)}, u32[]{:S(2)}) collective-permute-start(bf16[1,4,48,512]{3,2,1,0:T(8,128)(2,1)} %get-tuple-element.18), channel_id=1, source_target_pairs={{0,16},{8,24},{16,0},{24,8},{32,48},{40,56},{48,32},{56,40},{64,80... | collective-permute-start | bytes 589832 | tf_op jit(solution)/shard_map/ppermute | solution.py:141
  229.0 17.5 %collective-permute-start.2 = (bf16[1,4,48,512]{3,2,1,0:T(8,128)(2,1)}, bf16[1,4,48,512]{3,2,1,0:T(8,128)(2,1)S(1)}, u32[]{:S(2)}, u32[]{:S(2)}) collective-permute-start(bf16[1,4,48,512]{3,2,1,0:T(8,128)(2,1)} %get-tuple-element.17), channel_id=1, source_target_pairs={{0,24},{8,16},{16,8},{24,0},{32,56},{40,48},{48,40},{56,32},{64,88... | collective-permute-start | bytes 589832 | tf_op jit(solution)/shard_map/ppermute | solution.py:141
  229.3 21.9 %collective-permute-start.3 = (bf16[1,4,48,512]{3,2,1,0:T(8,128)(2,1)}, bf16[1,4,48,512]{3,2,1,0:T(8,128)(2,1)S(1)}, u32[]{:S(2)}, u32[]{:S(2)}) collective-permute-start(bf16[1,4,48,512]{3,2,1,0:T(8,128)(2,1)} %get-tuple-element.16), channel_id=1, source_target_pairs={{0,32},{8,40},{16,48},{24,56},{32,0},{40,8},{48,16},{56,24},{64,96... | collective-permute-start | bytes 589832 | tf_op jit(solution)/shard_map/ppermute | solution.py:141
  231.5 38.7 %collective-permute-start.4 = (bf16[1,4,48,512]{3,2,1,0:T(8,128)(2,1)}, bf16[1,4,48,512]{3,2,1,0:T(8,128)(2,1)S(1)}, u32[]{:S(2)}, u32[]{:S(2)}) collective-permute-start(bf16[1,4,48,512]{3,2,1,0:T(8,128)(2,1)} %get-tuple-element.15), channel_id=1, source_target_pairs={{0,40},{8,32},{16,56},{24,48},{32,8},{40,0},{48,24},{56,16},{64,10... | collective-permute-start | bytes 589832 | tf_op jit(solution)/shard_map/ppermute | solution.py:141
  233.7 37.2 %collective-permute-start.5 = (bf16[1,4,48,512]{3,2,1,0:T(8,128)(2,1)}, bf16[1,4,48,512]{3,2,1,0:T(8,128)(2,1)S(1)}, u32[]{:S(2)}, u32[]{:S(2)}) collective-permute-start(bf16[1,4,48,512]{3,2,1,0:T(8,128)(2,1)} %get-tuple-element.14), channel_id=1, source_target_pairs={{0,48},{8,56},{16,32},{24,40},{32,16},{40,24},{48,0},{56,8},{64,11... | collective-permute-start | bytes 589832 | tf_op jit(solution)/shard_map/ppermute | solution.py:141
  242.1 47.8 %collective-permute-start.6 = (bf16[1,4,48,512]{3,2,1,0:T(8,128)(2,1)}, bf16[1,4,48,512]{3,2,1,0:T(8,128)(2,1)S(1)}, u32[]{:S(2)}, u32[]{:S(2)}) collective-permute-start(bf16[1,4,48,512]{3,2,1,0:T(8,128)(2,1)} %get-tuple-element.13), channel_id=1, source_target_pairs={{0,56},{8,48},{16,40},{24,32},{32,24},{40,16},{48,8},{56,0},{64,12... | collective-permute-start | bytes 589832 | tf_op jit(solution)/shard_map/ppermute | solution.py:141
  246.5 45.4 %collective-permute-start.7 = (bf16[1,4,48,512]{3,2,1,0:T(8,128)(2,1)}, bf16[1,4,48,512]{3,2,1,0:T(8,128)(2,1)S(1)}, u32[]{:S(2)}, u32[]{:S(2)}) collective-permute-start(bf16[1,4,48,512]{3,2,1,0:T(8,128)(2,1)} %get-tuple-element.12), channel_id=1, source_target_pairs={{0,64},{8,72},{16,80},{24,88},{32,96},{40,104},{48,112},{56,120},{... | collective-permute-start | bytes 589832 | tf_op jit(solution)/shard_map/ppermute | solution.py:141
  251.2 42.6 %collective-permute-start.8 = (bf16[1,4,48,512]{3,2,1,0:T(8,128)(2,1)}, bf16[1,4,48,512]{3,2,1,0:T(8,128)(2,1)S(1)}, u32[]{:S(2)}, u32[]{:S(2)}) collective-permute-start(bf16[1,4,48,512]{3,2,1,0:T(8,128)(2,1)} %get-tuple-element.11), channel_id=1, source_target_pairs={{0,72},{8,64},{16,88},{24,80},{32,104},{40,96},{48,120},{56,112},{... | collective-permute-start | bytes 589832 | tf_op jit(solution)/shard_map/ppermute | solution.py:141
  270.2 25.3 %collective-permute-start.9 = (bf16[1,4,48,512]{3,2,1,0:T(8,128)(2,1)}, bf16[1,4,48,512]{3,2,1,0:T(8,128)(2,1)S(1)}, u32[]{:S(2)}, u32[]{:S(2)}) collective-permute-start(bf16[1,4,48,512]{3,2,1,0:T(8,128)(2,1)} %get-tuple-element.10), channel_id=1, source_target_pairs={{0,80},{8,88},{16,64},{24,72},{32,112},{40,120},{48,96},{56,104},{... | collective-permute-start | bytes 589832 | tf_op jit(solution)/shard_map/ppermute | solution.py:141
  270.9 46.0 %collective-permute-start.10 = (bf16[1,4,48,512]{3,2,1,0:T(8,128)(2,1)}, bf16[1,4,48,512]{3,2,1,0:T(8,128)(2,1)S(1)}, u32[]{:S(2)}, u32[]{:S(2)}) collective-permute-start(bf16[1,4,48,512]{3,2,1,0:T(8,128)(2,1)} %get-tuple-element.9), channel_id=1, source_target_pairs={{0,88},{8,80},{16,72},{24,64},{32,120},{40,112},{48,104},{56,96},{... | collective-permute-start | bytes 589832 | tf_op jit(solution)/shard_map/ppermute | solution.py:141
  289.8 31.3 %collective-permute-start.11 = (bf16[1,4,48,512]{3,2,1,0:T(8,128)(2,1)}, bf16[1,4,48,512]{3,2,1,0:T(8,128)(2,1)S(1)}, u32[]{:S(2)}, u32[]{:S(2)}) collective-permute-start(bf16[1,4,48,512]{3,2,1,0:T(8,128)(2,1)} %get-tuple-element.8), channel_id=1, source_target_pairs={{0,96},{8,104},{16,112},{24,120},{32,64},{40,72},{48,80},{56,88},{... | collective-permute-start | bytes 589832 | tf_op jit(solution)/shard_map/ppermute | solution.py:141
  291.9 33.3 %collective-permute-start.12 = (bf16[1,4,48,512]{3,2,1,0:T(8,128)(2,1)S(1)}, bf16[1,4,48,512]{3,2,1,0:T(8,128)(2,1)S(1)}, u32[]{:S(2)}, u32[]{:S(2)}) collective-permute-start(bf16[1,4,48,512]{3,2,1,0:T(8,128)(2,1)S(1)} %copy-done.5), channel_id=1, source_target_pairs={{0,104},{8,96},{16,120},{24,112},{32,72},{40,64},{48,88},{56,80},{... | collective-permute-start | bytes 589832 | tf_op jit(solution)/shard_map/ppermute | solution.py:141
  293.8 38.6 %collective-permute-start.13 = (bf16[1,4,48,512]{3,2,1,0:T(8,128)(2,1)S(1)}, bf16[1,4,48,512]{3,2,1,0:T(8,128)(2,1)S(1)}, u32[]{:S(2)}, u32[]{:S(2)}) collective-permute-start(bf16[1,4,48,512]{3,2,1,0:T(8,128)(2,1)S(1)} %copy-done.4), channel_id=1, source_target_pairs={{0,112},{8,120},{16,96},{24,104},{32,80},{40,88},{48,64},{56,72},{... | collective-permute-start | bytes 589832 | tf_op jit(solution)/shard_map/ppermute | solution.py:141
  295.5 40.3 %collective-permute-start.14 = (bf16[1,4,48,512]{3,2,1,0:T(8,128)(2,1)S(1)}, bf16[1,4,48,512]{3,2,1,0:T(8,128)(2,1)S(1)}, u32[]{:S(2)}, u32[]{:S(2)}) collective-permute-start(bf16[1,4,48,512]{3,2,1,0:T(8,128)(2,1)S(1)} %get-tuple-element.5), channel_id=1, source_target_pairs={{0,120},{8,112},{16,104},{24,96},{32,88},{40,80},{48,72},{56,64},{... | collective-permute-start | bytes 589832 | tf_op jit(solution)/shard_map/ppermute | solution.py:141
Sparse Core Ops, SparseCore 0:
  110.9 44.8 reduce-scatter.1
